TPU v7x, 16 devices: a whole 2x2x2 slice. The times are simulated.
16 devices in a mesh: tp: 2 (over z), pp: 8 (over y, x, core).
Axes of the slice: x: 2, y: 2, z: 2, core: 2. Of those that a mesh axis runs over, the one named last changes fastest.
Arguments:
- x_micro: bfloat16 [48, 1, 128, 2048], replicated
- ln1_gain: bfloat16 [8, 2048], P('pp')
- ln1_bias: bfloat16 [8, 2048], P('pp')
- w_qkv: bfloat16 [8, 2048, 16, 384], P('pp', None, 'tp')
- b_qkv: bfloat16 [8, 16, 384], P('pp', 'tp')
- w_dense: bfloat16 [8, 16, 128, 2048], P('pp', 'tp')
- b_dense: bfloat16 [8, 2048], P('pp')
- ln2_gain: bfloat16 [8, 2048], P('pp')
- ln2_bias: bfloat16 [8, 2048], P('pp')
- w_up: bfloat16 [8, 2048, 8192], P('pp', None, 'tp')
- b_up: bfloat16 [8, 8192], P('pp', 'tp')
- w_down: bfloat16 [8, 8192, 2048], P('pp', 'tp')
- b_down: bfloat16 [8, 2048], P('pp')
Outputs:
- output: bfloat16 [48, 1, 128, 2048], replicated
All inputs are finite; a program needn't handle non-finite values.
Results may differ from a plain program's by a relative error of at most 0.02.
Values are sent between devices in bfloat16 or wider.
A program may use at most 1 GiB of HBM per device.

v0:
```python
import jax
import jax.numpy as jnp
from jax import lax
from jax.sharding import PartitionSpec as P


def layer_norm(x_act, gain, bias):
    x_f32 = x_act.astype(jnp.float32)
    centered = x_f32 - jnp.mean(x_f32, axis=-1, keepdims=True)
    spread = jnp.mean(centered * centered, axis=-1, keepdims=True)
    normed = centered * lax.rsqrt(spread + 1e-5)
    return (normed * gain.astype(jnp.float32) + bias.astype(jnp.float32)).astype(jnp.bfloat16)


def rotary_tables(seq_len, rot_dims):
    inv_freq = 1.0 / (10000.0 ** (jnp.arange(0, rot_dims, 2).astype(jnp.float32) / rot_dims))
    angles = jnp.arange(seq_len).astype(jnp.float32)[:, None] * inv_freq[None, :]
    angles = jnp.concatenate([angles, angles], axis=-1)
    return jnp.cos(angles), jnp.sin(angles)


def apply_rotary(heads_in, cos_tab, sin_tab, rot_dims):
    half_rot = rot_dims // 2
    rot_part = heads_in[..., :rot_dims].astype(jnp.float32)
    rotated = jnp.concatenate([-rot_part[..., half_rot:], rot_part[..., :half_rot]], axis=-1)
    mixed = rot_part * cos_tab[:, None, :] + rotated * sin_tab[:, None, :]
    return jnp.concatenate([mixed.astype(jnp.bfloat16), heads_in[..., rot_dims:]], axis=-1)


def branch_sum(x_act, weights, cos_tab, sin_tab):
    ln1_gain, ln1_bias, w_qkv, b_qkv, w_dense, ln2_gain, ln2_bias, w_up, b_up, w_down = weights
    head_dim = w_dense.shape[1]
    rot_dims = head_dim // 4
    positions = jnp.arange(x_act.shape[1])
    ln_attn = layer_norm(x_act, ln1_gain, ln1_bias)
    qkv_proj = jnp.einsum("bsd,dhe->bshe", ln_attn, w_qkv, preferred_element_type=jnp.float32)
    qkv_proj = (qkv_proj + b_qkv.astype(jnp.float32)).astype(jnp.bfloat16)
    query = apply_rotary(qkv_proj[..., :head_dim], cos_tab, sin_tab, rot_dims)
    key_rot = apply_rotary(qkv_proj[..., head_dim:2 * head_dim], cos_tab, sin_tab, rot_dims)
    values = qkv_proj[..., 2 * head_dim:]
    scores = jnp.einsum("bqhd,bkhd->bhqk", query, key_rot, preferred_element_type=jnp.float32) * head_dim ** -0.5
    causal = positions[:, None] >= positions[None, :]
    probs = jax.nn.softmax(jnp.where(causal, scores, -1e30), axis=-1).astype(jnp.bfloat16)
    context = jnp.einsum("bhqk,bkhd->bqhd", probs, values, preferred_element_type=jnp.float32).astype(jnp.bfloat16)
    attn_part = jnp.einsum("bqhd,hde->bqe", context, w_dense, preferred_element_type=jnp.float32)
    ln_mlp = layer_norm(x_act, ln2_gain, ln2_bias)
    hidden = jnp.einsum("bsd,df->bsf", ln_mlp, w_up, preferred_element_type=jnp.float32) + b_up.astype(jnp.float32)
    hidden = jax.nn.gelu(hidden, approximate=False).astype(jnp.bfloat16)
    mlp_part = jnp.einsum("bsf,fd->bsd", hidden, w_down, preferred_element_type=jnp.float32)
    return attn_part + mlp_part


def solution(mesh):
    n_stages = mesh.shape["pp"]
    in_specs = (P(), P("pp", None), P("pp", None), P("pp", None, "tp", None), P("pp", "tp", None),
                P("pp", "tp", None, None), P("pp", None), P("pp", None), P("pp", None),
                P("pp", None, "tp"), P("pp", "tp"), P("pp", "tp", None), P("pp", None))

    def device_fn(x_micro, ln1_gain, ln1_bias, w_qkv, b_qkv, w_dense, b_dense, ln2_gain, ln2_bias, w_up, b_up, w_down, b_down):
        weights = (ln1_gain[0], ln1_bias[0], w_qkv[0], b_qkv[0], w_dense[0],
                   ln2_gain[0], ln2_bias[0], w_up[0], b_up[0], w_down[0])
        bias_sum = b_dense[0].astype(jnp.float32) + b_down[0].astype(jnp.float32)
        n_micro = x_micro.shape[0]
        cos_tab, sin_tab = rotary_tables(x_micro.shape[2], w_dense.shape[2] // 4)
        stage = lax.axis_index("pp")
        is_last = stage == n_stages - 1
        forward_pairs = [(source, source + 1) for source in range(n_stages - 1)]

        def run_layer(x_act):
            return branch_sum(x_act, weights, cos_tab, sin_tab).astype(jnp.bfloat16)

        def tick(step, carry):
            incoming, result = carry
            micro_id = step - stage
            valid = jnp.logical_and(micro_id >= 0, micro_id < n_micro)
            slot = jnp.clip(micro_id, 0, n_micro - 1)
            first_in = lax.dynamic_index_in_dim(x_micro, slot, 0, keepdims=False)
            x_act = jnp.where(stage == 0, first_in, incoming)
            tp_part = lax.cond(valid, run_layer, jnp.zeros_like, x_act)
            summed = lax.psum(tp_part, "tp")
            out_act = (x_act.astype(jnp.float32) + bias_sum + summed.astype(jnp.float32)).astype(jnp.bfloat16)
            current = lax.dynamic_index_in_dim(result, slot, 0, keepdims=False)
            keep = jnp.logical_and(valid, is_last)
            result = lax.dynamic_update_index_in_dim(result, jnp.where(keep, out_act, current), slot, 0)
            incoming = lax.ppermute(out_act, "pp", forward_pairs)
            return incoming, result

        start = (jnp.zeros(x_micro.shape[1:], jnp.bfloat16), jnp.zeros_like(x_micro))
        _, result = lax.fori_loop(0, n_micro + n_stages - 1, tick, start)
        return lax.psum(result, "pp")

    return jax.shard_map(device_fn, mesh=mesh, in_specs=in_specs, out_specs=P(), check_vma=False)
```

profile of v0, /device:TPU:0, one launch (start us, length us, event | category | flops | bytes accessed | tf_op | source)
XLA Modules:
  0.0 4440.0 jit_solution(5834644880805162638)
XLA Ops:
  35.4 4065.8 %while.16 = (s32[]{:T(128)}, bf16[1,128,2048]{2,1,0:T(8,128)(2,1)S(1)}, bf16[48,1,128,2048]{3,2,1,0:T(8,128)(2,1)}, pred[]{:T(512)}, s32[]{:T(128)}, /*index=5*/...) while((s32[]{:T(128)}, ...), condition=%wide.region_8.9_spmd, body=%wide.region_0.8_spmd.sunk | while | flops 6554778624 | bytes 72724488 | solution.py:89
  36.5 34.9 conditional.2
  104.2 34.9 conditional.2
  175.4 34.9 conditional.2
  248.8 34.9 conditional.2
  322.1 34.9 conditional.2
  396.4 34.9 conditional.2
  470.7 34.9 conditional.2
  544.9 34.9 conditional.2
  619.2 34.9 conditional.2
  693.5 34.9 conditional.2
  767.7 34.9 conditional.2
  842.0 34.9 conditional.2
  916.2 34.9 conditional.2
  990.5 34.9 conditional.2
  1213.3 34.9 conditional.2
  1287.5 34.9 conditional.2
  1361.8 34.9 conditional.2
  1436.0 34.9 conditional.2
  1510.3 34.9 conditional.2
  1584.5 34.9 conditional.2
  1658.8 34.9 conditional.2
  1955.8 34.9 conditional.2
  2030.1 34.9 conditional.2
  3591.5 66.0 %all-reduce.5.cloned.1.call-done = bf16[1,128,2048]{2,1,0:T(8,128)(2,1)} async-done(((bf16[1,128,2048]{2,1,0:T(8,128)(2,1)}), bf16[1,128,2048]{2,1,0:T(8,128)(2,1)}) %all-reduce.5.cloned.1.call-update) | async-done | bytes 524304 | tf_op jit(solution)/shard_map/while/body/eval_jaxpr/psum | solution.py:80
  3665.8 66.0 %all-reduce.5.cloned.1.call-done = bf16[1,128,2048]{2,1,0:T(8,128)(2,1)} async-done(((bf16[1,128,2048]{2,1,0:T(8,128)(2,1)}), bf16[1,128,2048]{2,1,0:T(8,128)(2,1)}) %all-reduce.5.cloned.1.call-update) | async-done | bytes 524304 | tf_op jit(solution)/shard_map/while/body/eval_jaxpr/psum | solution.py:80
  3740.0 66.0 %all-reduce.5.cloned.1.call-done = bf16[1,128,2048]{2,1,0:T(8,128)(2,1)} async-done(((bf16[1,128,2048]{2,1,0:T(8,128)(2,1)}), bf16[1,128,2048]{2,1,0:T(8,128)(2,1)}) %all-reduce.5.cloned.1.call-update) | async-done | bytes 524304 | tf_op jit(solution)/shard_map/while/body/eval_jaxpr/psum | solution.py:80
  3814.3 66.0 %all-reduce.5.cloned.1.call-done = bf16[1,128,2048]{2,1,0:T(8,128)(2,1)} async-done(((bf16[1,128,2048]{2,1,0:T(8,128)(2,1)}), bf16[1,128,2048]{2,1,0:T(8,128)(2,1)}) %all-reduce.5.cloned.1.call-update) | async-done | bytes 524304 | tf_op jit(solution)/shard_map/while/body/eval_jaxpr/psum | solution.py:80
  3888.5 66.0 %all-reduce.5.cloned.1.call-done = bf16[1,128,2048]{2,1,0:T(8,128)(2,1)} async-done(((bf16[1,128,2048]{2,1,0:T(8,128)(2,1)}), bf16[1,128,2048]{2,1,0:T(8,128)(2,1)}) %all-reduce.5.cloned.1.call-update) | async-done | bytes 524304 | tf_op jit(solution)/shard_map/while/body/eval_jaxpr/psum | solution.py:80
  3962.8 66.0 %all-reduce.5.cloned.1.call-done = bf16[1,128,2048]{2,1,0:T(8,128)(2,1)} async-done(((bf16[1,128,2048]{2,1,0:T(8,128)(2,1)}), bf16[1,128,2048]{2,1,0:T(8,128)(2,1)}) %all-reduce.5.cloned.1.call-update) | async-done | bytes 524304 | tf_op jit(solution)/shard_map/while/body/eval_jaxpr/psum | solution.py:80
  4037.0 59.0 %all-reduce.5.cloned.1.call-done = bf16[1,128,2048]{2,1,0:T(8,128)(2,1)} async-done(((bf16[1,128,2048]{2,1,0:T(8,128)(2,1)}), bf16[1,128,2048]{2,1,0:T(8,128)(2,1)}) %all-reduce.5.cloned.1.call-update) | async-done | bytes 524304 | tf_op jit(solution)/shard_map/while/body/eval_jaxpr/psum | solution.py:80
  4101.7 309.8 %all-reduce.3.cloned.1.call-done = bf16[48,1,128,2048]{3,2,1,0:T(8,128)(2,1)} async-done(((bf16[48,1,128,2048]{3,2,1,0:T(8,128)(2,1)}), bf16[48,1,128,2048]{3,2,1,0:T(8,128)(2,1)}) %all-reduce.3.cloned.1.call-update) | async-done | bytes 25165840 | tf_op jit(solution)/shard_map/psum | solution.py:90
  (1516 shorter events, 4526.5 us)
Async XLA Ops:
  321.0 69.1 %all-reduce.5.cloned.1.call-start = ((), (), s32[]{:S(2)}) async-start(), calls=%async_computation.1 | async-start | bytes 1048576 | tf_op jit(solution)/shard_map/while/body/eval_jaxpr/psum | solution.py:80
  395.3 69.2 %all-reduce.5.cloned.1.call-start = ((), (), s32[]{:S(2)}) async-start(), calls=%async_computation.1 | async-start | bytes 1048576 | tf_op jit(solution)/shard_map/while/body/eval_jaxpr/psum | solution.py:80
  469.6 69.2 %all-reduce.5.cloned.1.call-start = ((), (), s32[]{:S(2)}) async-start(), calls=%async_computation.1 | async-start | bytes 1048576 | tf_op jit(solution)/shard_map/while/body/eval_jaxpr/psum | solution.py:80
  618.1 69.1 %all-reduce.5.cloned.1.call-start = ((), (), s32[]{:S(2)}) async-start(), calls=%async_computation.1 | async-start | bytes 1048576 | tf_op jit(solution)/shard_map/while/body/eval_jaxpr/psum | solution.py:80
  692.3 69.1 %all-reduce.5.cloned.1.call-start = ((), (), s32[]{:S(2)}) async-start(), calls=%async_computation.1 | async-start | bytes 1048576 | tf_op jit(solution)/shard_map/while/body/eval_jaxpr/psum | solution.py:80
  766.6 69.1 %all-reduce.5.cloned.1.call-start = ((), (), s32[]{:S(2)}) async-start(), calls=%async_computation.1 | async-start | bytes 1048576 | tf_op jit(solution)/shard_map/while/body/eval_jaxpr/psum | solution.py:80
  840.9 69.1 %all-reduce.5.cloned.1.call-start = ((), (), s32[]{:S(2)}) async-start(), calls=%async_computation.1 | async-start | bytes 1048576 | tf_op jit(solution)/shard_map/while/body/eval_jaxpr/psum | solution.py:80
  915.1 69.1 %all-reduce.5.cloned.1.call-start = ((), (), s32[]{:S(2)}) async-start(), calls=%async_computation.1 | async-start | bytes 1048576 | tf_op jit(solution)/shard_map/while/body/eval_jaxpr/psum | solution.py:80
  989.4 69.1 %all-reduce.5.cloned.1.call-start = ((), (), s32[]{:S(2)}) async-start(), calls=%async_computation.1 | async-start | bytes 1048576 | tf_op jit(solution)/shard_map/while/body/eval_jaxpr/psum | solution.py:80
  1063.6 69.1 %all-reduce.5.cloned.1.call-start = ((), (), s32[]{:S(2)}) async-start(), calls=%async_computation.1 | async-start | bytes 1048576 | tf_op jit(solution)/shard_map/while/body/eval_jaxpr/psum | solution.py:80
  1137.9 69.1 %all-reduce.5.cloned.1.call-start = ((), (), s32[]{:S(2)}) async-start(), calls=%async_computation.1 | async-start | bytes 1048576 | tf_op jit(solution)/shard_map/while/body/eval_jaxpr/psum | solution.py:80
  1286.4 69.1 %all-reduce.5.cloned.1.call-start = ((), (), s32[]{:S(2)}) async-start(), calls=%async_computation.1 | async-start | bytes 1048576 | tf_op jit(solution)/shard_map/while/body/eval_jaxpr/psum | solution.py:80
  1360.7 69.1 %all-reduce.5.cloned.1.call-start = ((), (), s32[]{:S(2)}) async-start(), calls=%async_computation.1 | async-start | bytes 1048576 | tf_op jit(solution)/shard_map/while/body/eval_jaxpr/psum | solution.py:80
  1434.9 69.1 %all-reduce.5.cloned.1.call-start = ((), (), s32[]{:S(2)}) async-start(), calls=%async_computation.1 | async-start | bytes 1048576 | tf_op jit(solution)/shard_map/while/body/eval_jaxpr/psum | solution.py:80
  1509.2 69.1 %all-reduce.5.cloned.1.call-start = ((), (), s32[]{:S(2)}) async-start(), calls=%async_computation.1 | async-start | bytes 1048576 | tf_op jit(solution)/shard_map/while/body/eval_jaxpr/psum | solution.py:80
  1583.4 69.1 %all-reduce.5.cloned.1.call-start = ((), (), s32[]{:S(2)}) async-start(), calls=%async_computation.1 | async-start | bytes 1048576 | tf_op jit(solution)/shard_map/while/body/eval_jaxpr/psum | solution.py:80
  1954.7 69.1 %all-reduce.5.cloned.1.call-start = ((), (), s32[]{:S(2)}) async-start(), calls=%async_computation.1 | async-start | bytes 1048576 | tf_op jit(solution)/shard_map/while/body/eval_jaxpr/psum | solution.py:80
  2029.0 69.1 %all-reduce.5.cloned.1.call-start = ((), (), s32[]{:S(2)}) async-start(), calls=%async_computation.1 | async-start | bytes 1048576 | tf_op jit(solution)/shard_map/while/body/eval_jaxpr/psum | solution.py:80
  2103.2 69.1 %all-reduce.5.cloned.1.call-start = ((), (), s32[]{:S(2)}) async-start(), calls=%async_computation.1 | async-start | bytes 1048576 | tf_op jit(solution)/shard_map/while/body/eval_jaxpr/psum | solution.py:80
  2177.5 69.1 %all-reduce.5.cloned.1.call-start = ((), (), s32[]{:S(2)}) async-start(), calls=%async_computation.1 | async-start | bytes 1048576 | tf_op jit(solution)/shard_map/while/body/eval_jaxpr/psum | solution.py:80
  2251.7 69.1 %all-reduce.5.cloned.1.call-start = ((), (), s32[]{:S(2)}) async-start(), calls=%async_computation.1 | async-start | bytes 1048576 | tf_op jit(solution)/shard_map/while/body/eval_jaxpr/psum | solution.py:80
  2697.3 69.1 %all-reduce.5.cloned.1.call-start = ((), (), s32[]{:S(2)}) async-start(), calls=%async_computation.1 | async-start | bytes 1048576 | tf_op jit(solution)/shard_map/while/body/eval_jaxpr/psum | solution.py:80
  2771.5 69.1 %all-reduce.5.cloned.1.call-start = ((), (), s32[]{:S(2)}) async-start(), calls=%async_computation.1 | async-start | bytes 1048576 | tf_op jit(solution)/shard_map/while/body/eval_jaxpr/psum | solution.py:80
  2845.8 69.1 %all-reduce.5.cloned.1.call-start = ((), (), s32[]{:S(2)}) async-start(), calls=%async_computation.1 | async-start | bytes 1048576 | tf_op jit(solution)/shard_map/while/body/eval_jaxpr/psum | solution.py:80
  2920.1 69.1 %all-reduce.5.cloned.1.call-start = ((), (), s32[]{:S(2)}) async-start(), calls=%async_computation.1 | async-start | bytes 1048576 | tf_op jit(solution)/shard_map/while/body/eval_jaxpr/psum | solution.py:80
  2994.3 69.1 %all-reduce.5.cloned.1.call-start = ((), (), s32[]{:S(2)}) async-start(), calls=%async_computation.1 | async-start | bytes 1048576 | tf_op jit(solution)/shard_map/while/body/eval_jaxpr/psum | solution.py:80
  3365.6 69.1 %all-reduce.5.cloned.1.call-start = ((), (), s32[]{:S(2)}) async-start(), calls=%async_computation.1 | async-start | bytes 1048576 | tf_op jit(solution)/shard_map/while/body/eval_jaxpr/psum | solution.py:80
  3439.9 69.1 %all-reduce.5.cloned.1.call-start = ((), (), s32[]{:S(2)}) async-start(), calls=%async_computation.1 | async-start | bytes 1048576 | tf_op jit(solution)/shard_map/while/body/eval_jaxpr/psum | solution.py:80
  3514.1 69.1 %all-reduce.5.cloned.1.call-start = ((), (), s32[]{:S(2)}) async-start(), calls=%async_computation.1 | async-start | bytes 1048576 | tf_op jit(solution)/shard_map/while/body/eval_jaxpr/psum | solution.py:80
  3588.4 69.1 %all-reduce.5.cloned.1.call-start = ((), (), s32[]{:S(2)}) async-start(), calls=%async_computation.1 | async-start | bytes 1048576 | tf_op jit(solution)/shard_map/while/body/eval_jaxpr/psum | solution.py:80
  3662.6 69.1 %all-reduce.5.cloned.1.call-start = ((), (), s32[]{:S(2)}) async-start(), calls=%async_computation.1 | async-start | bytes 1048576 | tf_op jit(solution)/shard_map/while/body/eval_jaxpr/psum | solution.py:80
  4101.1 310.4 %all-reduce.3.cloned.1.call-start = ((), (), s32[]{:S(2)}) async-start(), calls=%async_computation | async-start | bytes 50331648 | tf_op jit(solution)/shard_map/psum | solution.py:90
  (136 other events, 1876.0 us)
Sparse Core Ops, SparseCore 0:
  432.2 32.1 all-reduce.4
  506.5 32.1 all-reduce.4
  655.1 32.1 all-reduce.4
  729.3 32.1 all-reduce.4
  803.6 32.1 all-reduce.4
  877.8 32.1 all-reduce.4
  952.1 32.1 all-reduce.4
  1026.3 32.1 all-reduce.4
  1100.6 32.1 all-reduce.4
  1174.9 32.1 all-reduce.4
  1249.1 32.1 all-reduce.4
  1323.4 32.1 all-reduce.4
  1397.6 32.1 all-reduce.4
  1471.9 32.1 all-reduce.4
  1546.1 32.1 all-reduce.4
  1620.4 32.1 all-reduce.4
  1694.6 32.1 all-reduce.4
  1768.9 32.1 all-reduce.4
  1843.2 32.1 all-reduce.4
  1917.4 32.1 all-reduce.4
  1991.7 32.1 all-reduce.4
  2065.9 32.1 all-reduce.4
  2140.2 32.1 all-reduce.4
  2214.4 32.1 all-reduce.4
  2288.7 32.1 all-reduce.4
  3591.1 66.3 all-reduce.4
  3665.7 65.9 all-reduce.4
  3739.7 66.3 all-reduce.4
  3814.2 65.9 all-reduce.4
  3888.2 66.3 all-reduce.4
  3962.7 65.9 all-reduce.4
  4037.0 58.9 all-reduce.4
  (23 shorter events, 726.3 us)
Sparse Core Ops, SparseCore 1:
  4105.3 306.2 all-reduce.2
where the time goes:
time: 4460 us; the launch traced here: 4440 us
  waiting for transfers between devices  2330 us (52%)
  matrix products  1320 us (30%)
  other arithmetic  488 us (11%)
  local copies, waits for them, and re-layouts  197 us (4%)
  starting transfers between devices  83 us (2%)
    psum x55, waiting for transfers between devices, tick(): summed = lax.psum(tp_part, 'tp')  1940 us
    dot_general x48, matrix products, branch_sum(): jnp.einsum('bsf,fd->bsd', hidden, w_down, preferred_element_type=jnp.floa...  745 us
    dot_general x48, matrix products, branch_sum(): jnp.einsum('bsd,dhe->bshe', ln_attn, w_qkv, preferred_element_type=jnp.fl...  312 us
    psum x1, waiting for transfers between devices, device_fn(): return lax.psum(result, 'pp')  310 us
    dot_general x48, matrix products, branch_sum(): jnp.einsum('bqhd,hde->bqe', context, w_dense, preferred_element_type=jnp....  151 us
    dynamic_update_slice x55, other arithmetic, tick(): lax.dynamic_update_index_in_dim(result, jnp.where(keep, out_act, current)...  117 us
    sub x48, matrix products, branch_sum(): jax.nn.softmax(jnp.where(causal, scores, -1e+30), axis=-1)  109 us
  transfers between devices with their start and end apart: 111, of which 111 were waited for; matrix products, arithmetic and copies ran while one was open for 1% of the time, Pallas kernels for 0%

commit v1 on v0

v1 whole, which is shorter than its diff:
```python
import functools

import jax
import jax.numpy as jnp
import numpy as np
from jax import lax
from jax.experimental import pallas as pl
from jax.experimental.pallas import tpu as pltpu
from jax.sharding import PartitionSpec as P

MESH = pl.DeviceIdType.MESH
F32, BF16 = jnp.float32, jnp.bfloat16
X_SLOTS = 3
CHUNKS = 4
EAGER = 0


def rotary_lanes(seq_len, head_dim):
    rot = head_dim // 4
    half = rot // 2
    inv_freq = (1.0 / (np.float32(10000.0) ** (np.arange(0, rot, 2).astype(np.float32) / np.float32(rot)))).astype(np.float32)
    angles = np.arange(seq_len).astype(np.float32)[:, None] * inv_freq[None, :]
    cos, sin = np.cos(angles.astype(np.float64)), np.sin(angles.astype(np.float64))
    cos_l = np.ones((seq_len, head_dim), np.float32)
    sin_lo = np.zeros((seq_len, head_dim), np.float32)
    sin_hi = np.zeros((seq_len, head_dim), np.float32)
    cos_l[:, :half], cos_l[:, half:rot] = cos, cos
    sin_lo[:, :half] = -sin
    sin_hi[:, half:rot] = sin
    return cos_l, sin_lo, sin_hi


def kernel(dims, x_hbm, cos_ref, slo_ref, shi_ref, g1_ref, b1_ref, g2_ref, b2_ref, bqkv_ref, bup_ref, bd_ref, bdn_ref,
           wqkv_hbm, wd_hbm, wup_hbm, wdn_hbm, y_hbm,
           wqkv, wd, wup, wdn, xin, psend, precv, osend, a_ref, c_ref, qkv, ctx, hid, g1, b1, g2, b2, bqkv, bup, bias,
           w_sem, x_ls, x_rs, x_free, p_ss, p_rs, f_ss, b_ss, r_ss, y_rs):
    n_micro, n_st, seq, d, heads, hd, ffn = dims
    S, C = X_SLOTS, CHUNKS
    cw = d // C
    tp, st = lax.axis_index("tp"), lax.axis_index("pp")
    is_first, is_last = st == 0, st == n_st - 1
    not_first, not_last = st > 0, st < n_st - 1
    partner = (1 - tp, st)

    def cols(c):
        return pl.ds(c * cw, cw)

    w_copies = [pltpu.make_async_copy(src, dst, w_sem.at[k])
                for k, (src, dst) in enumerate(((wqkv_hbm, wqkv), (wup_hbm, wup), (wd_hbm, wd), (wdn_hbm, wdn)))]

    def x_load(m):
        s = lax.rem(m, S)
        return pltpu.make_async_copy(x_hbm.at[m], xin.at[s], x_ls.at[s])

    @pl.when(is_first)
    def _():
        for m in range(S):
            x_load(m).start()

    for cp in w_copies:
        cp.start()

    def p_copy(m, c):
        s = lax.rem(m, 2)
        return pltpu.make_async_remote_copy(psend.at[s, :, cols(c)], precv.at[s, :, cols(c)], p_ss.at[s, c], p_rs.at[s, c],
                                            device_id=partner, device_id_type=MESH)

    def f_copy(m, c):
        s, xs = lax.rem(m, 2), lax.rem(m, S)
        return pltpu.make_async_remote_copy(osend.at[s, :, cols(c)], xin.at[xs, :, cols(c)], f_ss.at[s, c], x_rs.at[xs, c],
                                            device_id=(tp, st + 1), device_id_type=MESH)

    def b_copies(m):
        s = lax.rem(m, 2)
        far = [pltpu.make_async_remote_copy(osend.at[s], y_hbm.at[m], b_ss.at[s, k], y_rs.at[m],
                                            device_id=(tp, target), device_id_type=MESH)
               for k, target in enumerate((n_st - 3, n_st - 5, n_st - 2))]
        return far + [pltpu.make_async_copy(osend.at[s], y_hbm.at[m], b_ss.at[s, 3])]

    def y_wait(m):
        pltpu.make_async_remote_copy(y_hbm.at[m], y_hbm.at[m], r_ss.at[0], y_rs.at[m],
                                     device_id=partner, device_id_type=MESH).wait_recv()

    def relay_copy(m, k, target):
        return pltpu.make_async_remote_copy(y_hbm.at[m], y_hbm.at[m], r_ss.at[k], y_rs.at[m],
                                            device_id=(tp, target), device_id_type=MESH)

    two_hop = st == n_st - 3
    relays = jnp.logical_and(lax.rem(st, 2) == 1, not_last)

    def relay(m):
        y_wait(m)

        @pl.when(m > 0)
        def _():
            relay_copy(m - 1, 0, st - 1).wait_send()

        relay_copy(m, 0, st - 1).start()

        @pl.when(two_hop)
        def _():
            @pl.when(m > 0)
            def _():
                relay_copy(m - 1, 1, 1).wait_send()

            relay_copy(m, 1, 1).start()

    delay = 3 + ((n_st - 1 - st) * 3) // 2

    for src, dst in ((g1_ref, g1), (b1_ref, b1), (g2_ref, g2), (b2_ref, b2), (bqkv_ref, bqkv), (bup_ref, bup)):
        dst[...] = src[...].astype(F32)
    bias[...] = bd_ref[...].astype(F32) + bdn_ref[...].astype(F32)

    def finish_chunk(m, c):
        s, xs = lax.rem(m, 2), lax.rem(m, S)
        p_copy(m, c).wait()

        @pl.when(m >= 2)
        def _():
            @pl.when(not_last)
            def _():
                f_copy(m - 2, c).wait_send()

            if c == 0:
                @pl.when(is_last)
                def _():
                    far = b_copies(m - 2)
                    for cp in far[:-1]:
                        cp.wait_send()
                    far[-1].wait()

        both = psend[s, :, cols(c)].astype(F32) + precv[s, :, cols(c)].astype(F32)
        base = xin[xs, :, cols(c)].astype(F32) + bias[:, cols(c)]
        osend[s, :, cols(c)] = (base + both).astype(BF16)

        @pl.when(not_last)
        def _():
            if c == 0:
                @pl.when(m >= S)
                def _():
                    pl.semaphore_wait(x_free, 1)
            f_copy(m, c).start()

        if c == C - 1:
            @pl.when(is_last)
            def _():
                for cp in b_copies(m):
                    cp.start()

            @pl.when(m + S < n_micro)
            def _():
                @pl.when(not_first)
                def _():
                    pl.semaphore_signal(x_free, inc=1, device_id=(tp, st - 1), device_id_type=MESH)

                @pl.when(is_first)
                def _():
                    x_load(m + S).start()

    def front(i):
        xs = lax.rem(i, S)
        rows_per = 16
        for r in range(seq // rows_per):
            rows = pl.ds(r * rows_per, rows_per)
            x_f32 = xin[xs, rows, :].astype(F32)
            centered = x_f32 - jnp.mean(x_f32, axis=-1, keepdims=True)
            spread = jnp.mean(centered * centered, axis=-1, keepdims=True)
            normed = centered * lax.rsqrt(spread + 1e-5)
            a_ref[rows, :] = (normed * g1[...] + b1[...]).astype(BF16)
            c_ref[rows, :] = (normed * g2[...] + b2[...]).astype(BF16)

        a = a_ref[...]
        qw = 2 * 3 * hd
        lane = lax.broadcasted_iota(jnp.int32, (seq, hd), 1)
        rot = hd // 4
        for q in range(heads * 3 * hd // qw):
            cs = pl.ds(q * qw, qw)
            part = jnp.dot(a, wqkv[:, cs], preferred_element_type=F32)
            qkv[:, cs] = (part + bqkv[:, cs]).astype(BF16)

        def rotate(v):
            v = v.astype(F32)
            mixed = v * cos_ref[...] + (pltpu.roll(v, hd - rot // 2, 1) * slo_ref[...] + pltpu.roll(v, rot // 2, 1) * shi_ref[...])
            return jnp.where(lane < rot, mixed, v).astype(BF16)

        causal = lax.broadcasted_iota(jnp.int32, (seq, seq), 0) >= lax.broadcasted_iota(jnp.int32, (seq, seq), 1)
        for h in range(heads):
            base = h * 3 * hd
            query = rotate(qkv[:, pl.ds(base, hd)])
            key = rotate(qkv[:, pl.ds(base + hd, hd)])
            value = qkv[:, pl.ds(base + 2 * hd, hd)]
            scores = lax.dot_general(query, key, (((1,), (1,)), ((), ())), preferred_element_type=F32) * hd ** -0.5
            scores = jnp.where(causal, scores, -1e30)
            top = jnp.max(scores, axis=-1, keepdims=True)
            e = jnp.exp(scores - top)
            probs = (e / jnp.sum(e, axis=-1, keepdims=True)).astype(BF16)
            ctx[:, pl.ds(h * hd, hd)] = jnp.dot(probs, value, preferred_element_type=F32).astype(BF16)

        c = c_ref[...]
        uw = 512
        for u in range(ffn // uw):
            cs = pl.ds(u * uw, uw)
            up = jnp.dot(c, wup[:, cs], preferred_element_type=F32) + bup[:, cs]
            gelu = 0.5 * up * (1.0 + lax.erf(up * np.float32(np.sqrt(0.5))))
            hid[:, cs] = gelu.astype(BF16)

    def back_chunk(i, c):
        part = jnp.dot(hid[...], wdn[:, cols(c)], preferred_element_type=F32)
        part = part + jnp.dot(ctx[...], wd[:, cols(c)], preferred_element_type=F32)
        psend[lax.rem(i, 2), :, cols(c)] = part.astype(BF16)
        p_copy(i, c).start()

    w_copies[0].wait()
    w_copies[1].wait()

    def body(i, carry):
        @pl.when(is_first)
        def _():
            x_load(i).wait()

        @pl.when(not_first)
        def _():
            for c in range(C):
                f_copy(i, c).wait_recv()

        front(i)

        @pl.when(i == 0)
        def _():
            w_copies[2].wait()
            w_copies[3].wait()

        for c in range(C):
            @pl.when(i - 1 >= EAGER)
            def _():
                finish_chunk(i - 1, c)

            back_chunk(i, c)

        @pl.when(i < EAGER)
        def _():
            for c in range(C):
                finish_chunk(i, c)

        @pl.when(jnp.logical_and(relays, i >= delay))
        def _():
            relay(i - delay)

        return carry

    lax.fori_loop(0, n_micro, body, 0)
    last = n_micro - 1
    for c in range(C):
        finish_chunk(last, c)

    @pl.when(not_last)
    def _():
        for m in (n_micro - 2, n_micro - 1):
            for c in range(C):
                f_copy(m, c).wait_send()

    @pl.when(is_last)
    def _():
        for m in (n_micro - 2, n_micro - 1):
            far = b_copies(m)
            for cp in far[:-1]:
                cp.wait_send()
            far[-1].wait()

    @pl.when(relays)
    def _():
        def more(m, carry):
            relay(m)
            return carry

        lax.fori_loop(jnp.maximum(n_micro - delay, 0), n_micro, more, 0)
        relay_copy(last, 0, st - 1).wait_send()

        @pl.when(two_hop)
        def _():
            relay_copy(last, 1, 1).wait_send()

    @pl.when(lax.rem(st, 2) == 0)
    def _():
        def leaf(m, carry):
            y_wait(m)
            return carry

        lax.fori_loop(0, n_micro, leaf, 0)


def solution(mesh):
    n_st = mesh.shape["pp"]
    in_specs = (P(), P("pp", None), P("pp", None), P("pp", None, "tp", None), P("pp", "tp", None),
                P("pp", "tp", None, None), P("pp", None), P("pp", None), P("pp", None),
                P("pp", None, "tp"), P("pp", "tp"), P("pp", "tp", None), P("pp", None))

    def device_fn(x_micro, ln1_gain, ln1_bias, w_qkv, b_qkv, w_dense, b_dense, ln2_gain, ln2_bias, w_up, b_up, w_down, b_down):
        n_micro, _, seq, d = x_micro.shape
        heads, hd = w_dense.shape[1], w_dense.shape[2]
        ffn = w_up.shape[2]
        cos_l, sin_lo, sin_hi = rotary_lanes(seq, hd)
        dims = (n_micro, n_st, seq, d, heads, hd, ffn)
        vm = pl.BlockSpec(memory_space=pltpu.VMEM)
        hbm = pl.BlockSpec(memory_space=pl.ANY)
        dma = pltpu.SemaphoreType.DMA
        S, C = X_SLOTS, CHUNKS
        out = pl.pallas_call(
            functools.partial(kernel, dims),
            out_shape=jax.ShapeDtypeStruct((n_micro, seq, d), BF16),
            in_specs=[hbm] + [vm] * 11 + [hbm] * 4,
            out_specs=hbm,
            scratch_shapes=[
                pltpu.VMEM((d, heads * 3 * hd), BF16), pltpu.VMEM((heads * hd, d), BF16),
                pltpu.VMEM((d, ffn), BF16), pltpu.VMEM((ffn, d), BF16),
                pltpu.VMEM((S, seq, d), BF16), pltpu.VMEM((2, seq, d), BF16), pltpu.VMEM((2, seq, d), BF16),
                pltpu.VMEM((2, seq, d), BF16),
                pltpu.VMEM((seq, d), BF16), pltpu.VMEM((seq, d), BF16),
                pltpu.VMEM((seq, heads * 3 * hd), BF16), pltpu.VMEM((seq, heads * hd), BF16), pltpu.VMEM((seq, ffn), BF16),
                pltpu.VMEM((1, d), F32), pltpu.VMEM((1, d), F32), pltpu.VMEM((1, d), F32), pltpu.VMEM((1, d), F32),
                pltpu.VMEM((1, heads * 3 * hd), F32), pltpu.VMEM((1, ffn), F32), pltpu.VMEM((1, d), F32),
                dma((4,)), dma((S,)), dma((S, C)), pltpu.SemaphoreType.REGULAR,
                dma((2, C)), dma((2, C)), dma((2, C)), dma((2, 4)), dma((2,)), dma((n_micro,)),
            ],
            compiler_params=pltpu.CompilerParams(has_side_effects=True, vmem_limit_bytes=67_043_328),
            name="neox_pipeline",
        )(x_micro.reshape(n_micro, seq, d), jnp.asarray(cos_l), jnp.asarray(sin_lo), jnp.asarray(sin_hi),
          ln1_gain, ln1_bias, ln2_gain, ln2_bias, b_qkv.reshape(1, -1), b_up, b_dense, b_down,
          w_qkv.reshape(d, heads * 3 * hd), w_dense.reshape(heads * hd, d), w_up[0], w_down[0])
        return out.reshape(x_micro.shape)

    return jax.shard_map(device_fn, mesh=mesh, in_specs=in_specs, out_specs=P(), check_vma=False)
```

time: 4460 us -> 1200 us (0.27)
  waiting for transfers between devices: 2330 us -> 0 us
  matrix products: 1320 us -> 0 us
  Pallas kernels: 0 us -> 1170 us
  other arithmetic: 488 us -> 0 us
  local copies, waits for them, and re-layouts: 197 us -> 34.2 us
  starting transfers between devices: 83 us -> 0 us
    psum x56 -> x0, waiting for transfers between devices: 2250 us -> none  [the longest x55 1940 us: tick(): summed = lax.psum(tp_part, 'tp')]
    dot_general x144 -> x0, matrix products: 1210 us -> none  [the longest x48 745 us: branch_sum(): jnp.einsum('bsf,fd->bsd', hidden, w_down, preferred_element_type=jnp.floa...]
    pallas_call x0 -> x1, Pallas kernels: none -> 1170 us  [device_fn(): pl.pallas_call(functools.partial(kernel, dims), out_shape=jax.ShapeDtypeS...]
    convert_element_type x385 -> x0, other arithmetic: 263 us -> none  [the longest x96 66 us: layer_norm(): gain.astype(jnp.float32)]
    dynamic_update_slice x55 -> x0, other arithmetic: 117 us -> none  [tick(): lax.dynamic_update_index_in_dim(result, jnp.where(keep, out_act, current)...]
    sub x48 -> x0, matrix products: 109 us -> none  [branch_sum(): jax.nn.softmax(jnp.where(causal, scores, -1e+30), axis=-1)]
    ppermute x55 -> x0, starting transfers between devices: 82.9 us -> none  [tick(): incoming = lax.ppermute(out_act, 'pp', forward_pairs)]
    ppermute x55 -> x0, waiting for transfers between devices: 81.5 us -> none  [tick(): incoming = lax.ppermute(out_act, 'pp', forward_pairs)]
  transfers between devices with their start and end apart: 111 -> 0, of which waited for: 111 -> 0; matrix products, arithmetic and copies ran while one was open for 1% -> 0% of each run, Pallas kernels for 0% -> 0%
where the time goes in v1:
time: 1200 us
  Pallas kernels  1170 us (98%)
  local copies, waits for them, and re-layouts  34.2 us (3%)
    pallas_call x1, Pallas kernels, device_fn(): pl.pallas_call(functools.partial(kernel, dims), out_shape=jax.ShapeDtypeS...  1170 us
    unnamed x3, local copies, waits for them, and re-layouts  34.2 us

profile of v1, /device:TPU:0, one launch (start us, length us, event | category | flops | bytes accessed | tf_op | source)
XLA Modules:
  0.0 1202.9 jit_solution(9289004957469196975)
XLA Ops:
  0.0 1.3 copy.18
  1.3 11.9 copy.19
  13.2 1168.7 %neox_pipeline.1 = bf16[48,128,2048]{2,1,0:T(8,128)(2,1)} custom-call(bf16[48,128,2048]{2,1,0:T(8,128)(2,1)} %bitcast.14, f32[128,128]{1,0:T(8,128)} %constant.6.clone.cos_ref, f32[128,128]{1,0:T(8,128)} %constant.7.clone.slo_ref, f32[128,128]{1,0:T(8,128)} %constant.8.clone.shi_ref, bf16[1,2048]{1,0:T(2,128)(2,1)} %g1_ref.1, bf16[1,2048]{1,0:T(2,128)(2,1)} %b1_ref.1, ...), custom_call_target="tpu_custom_call" | custom-call | tf_op jit(solution)/shard_map/neox_pipeline/pallas_call | solution.py:308
  1181.8 21.0 %copy.21 = bf16[48,1,128,2048]{3,2,1,0:T(8,128)(2,1)} copy(bf16[48,1,128,2048]{3,2,1,0:T(8,128)(2,1)} %bitcast.12) | data formatting | bytes 50331648

commit v2 on v1

v2 whole, which is shorter than its diff:
```python
import functools

import jax
import jax.numpy as jnp
import numpy as np
from jax import lax
from jax.experimental import pallas as pl
from jax.experimental.pallas import tpu as pltpu
from jax.sharding import PartitionSpec as P

MESH = pl.DeviceIdType.MESH
F32, BF16 = jnp.float32, jnp.bfloat16
X_SLOTS = 4
CHUNKS = 4
SUM_AT = (1, 1, 3, 3)
K_BLOCK = 128


def rotary_lanes(seq_len, head_dim):
    rot = head_dim // 4
    half = rot // 2
    inv_freq = (1.0 / (np.float32(10000.0) ** (np.arange(0, rot, 2).astype(np.float32) / np.float32(rot)))).astype(np.float32)
    angles = np.arange(seq_len).astype(np.float32)[:, None] * inv_freq[None, :]
    cos, sin = np.cos(angles.astype(np.float64)), np.sin(angles.astype(np.float64))
    cos_l = np.ones((seq_len, head_dim), np.float32)
    sin_lo = np.zeros((seq_len, head_dim), np.float32)
    sin_hi = np.zeros((seq_len, head_dim), np.float32)
    cos_l[:, :half], cos_l[:, half:rot] = cos, cos
    sin_lo[:, :half] = -sin
    sin_hi[:, half:rot] = sin
    return cos_l, sin_lo, sin_hi


def kernel(dims, x_hbm, cos_ref, slo_ref, shi_ref, g1_ref, b1_ref, g2_ref, b2_ref, bqkv_ref, bup_ref, bd_ref, bdn_ref,
           wqkv_hbm, wd_hbm, wup_hbm, wdn_hbm, y_hbm,
           wq_in, wq_f32, wqkv, wd, wup, wdn, xin, psend, precv, osend, a_ref, c_ref, qkv, probs, ctx, hid, g1, b1, g2, b2, bqkv, bup, bias,
           w_sem, wq_sem, x_ls, x_rs, x_free, p_ss, p_rs, f_ss, b_ss, r_ss, y_rs):
    n_micro, n_st, seq, d, heads, hd, ffn = dims
    S, C = X_SLOTS, CHUNKS
    cw = d // C
    tp, st = lax.axis_index("tp"), lax.axis_index("pp")
    is_first, is_last = st == 0, st == n_st - 1
    not_first, not_last = st > 0, st < n_st - 1
    partner = (1 - tp, st)

    def cols(c):
        return pl.ds(c * cw, cw)

    def w_copy(k):
        src, dst = ((wup_hbm, wup), (wd_hbm, wd), (wdn_hbm, wdn))[k]
        return pltpu.make_async_copy(src, dst, w_sem.at[k])

    def wq_load(kb):
        return pltpu.make_async_copy(wqkv_hbm.at[pl.ds(kb * K_BLOCK, K_BLOCK)], wq_in.at[lax.rem(kb, 2)], wq_sem.at[lax.rem(kb, 2)])

    def x_load(m):
        s = lax.rem(m, S)
        return pltpu.make_async_copy(x_hbm.at[m], xin.at[s], x_ls.at[s])

    @pl.when(is_first)
    def _():
        for m in range(S):
            x_load(m).start()

    wq_load(0).start()
    wq_load(1).start()

    def p_copy(m, c):
        s = lax.rem(m, 2)
        return pltpu.make_async_remote_copy(psend.at[s, :, cols(c)], precv.at[s, :, cols(c)], p_ss.at[s, c], p_rs.at[s, c],
                                            device_id=partner, device_id_type=MESH)

    def f_copy(m, c):
        s, xs = lax.rem(m, 2), lax.rem(m, S)
        return pltpu.make_async_remote_copy(osend.at[s, :, cols(c)], xin.at[xs, :, cols(c)], f_ss.at[s, c], x_rs.at[xs, c],
                                            device_id=(tp, st + 1), device_id_type=MESH)

    def b_copies(m, c):
        s = lax.rem(m, 2)
        src, dst = osend.at[s, :, cols(c)], y_hbm.at[m, :, cols(c)]
        far = [pltpu.make_async_remote_copy(src, dst, b_ss.at[s, k, c], y_rs.at[m, c], device_id=(tp, target), device_id_type=MESH)
               for k, target in enumerate((n_st - 3, n_st - 5, n_st - 2))]
        return far + [pltpu.make_async_copy(src, dst, b_ss.at[s, 3, c])]

    def b_wait(m, c):
        copies = b_copies(m, c)
        for cp in copies[:-1]:
            cp.wait_send()
        copies[-1].wait()

    def relay_copy(m, c, k, target):
        here = y_hbm.at[m, :, cols(c)]
        return pltpu.make_async_remote_copy(here, here, r_ss.at[k, c], y_rs.at[m, c], device_id=(tp, target), device_id_type=MESH)

    def y_wait(m, c):
        relay_copy(m, c, 0, 0).wait_recv()

    two_hop = st == n_st - 3
    relays = jnp.logical_and(lax.rem(st, 2) == 1, not_last)

    def relay(m):
        for c in range(C):
            y_wait(m, c)

            @pl.when(m > 0)
            def _():
                relay_copy(m - 1, c, 0, st - 1).wait_send()

            relay_copy(m, c, 0, st - 1).start()

            @pl.when(two_hop)
            def _():
                @pl.when(m > 0)
                def _():
                    relay_copy(m - 1, c, 1, 1).wait_send()

                relay_copy(m, c, 1, 1).start()

    ahead = n_st - 1 - st
    delay = 4 + ahead + (ahead * ahead + 2) // 3

    for src, dst in ((g1_ref, g1), (b1_ref, b1), (g2_ref, g2), (b2_ref, b2), (bup_ref, bup)):
        dst[...] = src[...].astype(F32)
    for h in range(heads):
        bqkv[:, pl.ds(h * 3 * hd, 3 * hd)] = bqkv_ref[pl.ds(h, 1), :].astype(F32)
    bias[...] = bd_ref[...].astype(F32) + bdn_ref[...].astype(F32)

    n_kb = d // K_BLOCK
    up_rows = d // n_kb

    def lay_out(kb, carry):
        rows = pl.ds(pl.multiple_of(kb * K_BLOCK, K_BLOCK), K_BLOCK)
        up_r = pl.ds(kb * up_rows, up_rows)
        pltpu.make_async_copy(wup_hbm.at[up_r], wup.at[up_r], w_sem.at[0]).start()
        wq_load(kb).wait()
        for e in range(3 * hd // 128):
            wq_f32[e] = wq_in[lax.rem(kb, 2), :, :, pl.ds(e * 128, 128)].astype(F32).reshape(K_BLOCK * heads, 128)

        @pl.when(kb + 2 < n_kb)
        def _():
            wq_load(kb + 2).start()

        for h in range(heads):
            for e in range(3 * hd // 128):
                wqkv[rows, pl.ds(h * 3 * hd + e * 128, 128)] = wq_f32[e, pl.ds(h, K_BLOCK, stride=heads), :].astype(BF16)
        return carry

    def finish_chunk(m, c):
        s, xs = lax.rem(m, 2), lax.rem(m, S)
        p_copy(m, c).wait()

        @pl.when(m >= 2)
        def _():
            @pl.when(not_last)
            def _():
                f_copy(m - 2, c).wait_send()

            @pl.when(is_last)
            def _():
                b_wait(m - 2, c)

        both = psend[s, :, cols(c)].astype(F32) + precv[s, :, cols(c)].astype(F32)
        base = xin[xs, :, cols(c)].astype(F32) + bias[:, cols(c)]
        osend[s, :, cols(c)] = (base + both).astype(BF16)

        @pl.when(not_last)
        def _():
            if c == 0:
                @pl.when(m >= S)
                def _():
                    pl.semaphore_wait(x_free, 1)
            f_copy(m, c).start()

        @pl.when(is_last)
        def _():
            for cp in b_copies(m, c):
                cp.start()

        if c == C - 1:
            @pl.when(m + S < n_micro)
            def _():
                @pl.when(not_first)
                def _():
                    pl.semaphore_signal(x_free, inc=1, device_id=(tp, st - 1), device_id_type=MESH)

                @pl.when(is_first)
                def _():
                    x_load(m + S).start()

    def attention_part(i):
        xs = lax.rem(i, S)
        rows_per = 16
        for r in range(seq // rows_per):
            rows = pl.ds(r * rows_per, rows_per)
            x_f32 = xin[xs, rows, :].astype(F32)
            centered = x_f32 - jnp.mean(x_f32, axis=-1, keepdims=True)
            spread = jnp.mean(centered * centered, axis=-1, keepdims=True)
            normed = centered * lax.rsqrt(spread + 1e-5)
            a_ref[rows, :] = (normed * g1[...] + b1[...]).astype(BF16)
            c_ref[rows, :] = (normed * g2[...] + b2[...]).astype(BF16)

        a = a_ref[...]
        qw = 2 * 3 * hd
        lane = lax.broadcasted_iota(jnp.int32, (seq, hd), 1)
        rot = hd // 4
        def rotate(v):
            v = v.astype(F32)
            mixed = v * cos_ref[...] + (pltpu.roll(v, hd - rot // 2, 1) * slo_ref[...] + pltpu.roll(v, rot // 2, 1) * shi_ref[...])
            return jnp.where(lane < rot, mixed, v).astype(BF16)

        causal = lax.broadcasted_iota(jnp.int32, (seq, seq), 0) >= lax.broadcasted_iota(jnp.int32, (seq, seq), 1)
        def head_probs(h):
            base = h * 3 * hd
            query = rotate(qkv[:, pl.ds(base, hd)])
            key = rotate(qkv[:, pl.ds(base + hd, hd)])
            scores = lax.dot_general(query, key, (((1,), (1,)), ((), ())), preferred_element_type=F32) * hd ** -0.5
            scores = jnp.where(causal, scores, -1e30)
            top = jnp.max(scores, axis=-1, keepdims=True)
            e = jnp.exp(scores - top)
            probs[h] = (e / jnp.sum(e, axis=-1, keepdims=True)).astype(BF16)

        n_q = heads * 3 * hd // qw
        for q in range(n_q + 1):
            if q < n_q:
                cs = pl.ds(q * qw, qw)
                part = jnp.dot(a, wqkv[:, cs], preferred_element_type=F32)
                qkv[:, cs] = (part + bqkv[:, cs]).astype(BF16)
            if q > 0:
                for h in range(2 * (q - 1), 2 * q):
                    head_probs(h)

    def up_part(part):
        c = c_ref[...]
        uw = 512
        half = ffn // uw // 2
        for u in range(part * half, (part + 1) * half):
            cs = pl.ds(u * uw, uw)
            up = jnp.dot(c, wup[:, cs], preferred_element_type=F32) + bup[:, cs]
            gelu = 0.5 * up * (1.0 + lax.erf(up * np.float32(np.sqrt(0.5))))
            hid[:, cs] = gelu.astype(BF16)
            n_u = ffn // uw
            for h in range(heads):
                if u == min(1 + h * n_u // heads, n_u - 1):
                    value = qkv[:, pl.ds(h * 3 * hd + 2 * hd, hd)]
                    ctx[:, pl.ds(h * hd, hd)] = jnp.dot(probs[h], value, preferred_element_type=F32).astype(BF16)

    def back_chunk(i, c):
        part = jnp.dot(hid[...], wdn[:, cols(c)], preferred_element_type=F32)
        part = part + jnp.dot(ctx[...], wd[:, cols(c)], preferred_element_type=F32)
        psend[lax.rem(i, 2), :, cols(c)] = part.astype(BF16)
        p_copy(i, c).start()

    lax.fori_loop(0, n_kb, lay_out, 0)
    w_copy(1).start()
    w_copy(2).start()

    def body(i, carry):
        def sums(where):
            here = [c for c in range(C) if SUM_AT[c] == where]
            if here:
                @pl.when(i > 0)
                def _():
                    for c in here:
                        finish_chunk(i - 1, c)

        sums(0)

        @pl.when(is_first)
        def _():
            x_load(i).wait()

        @pl.when(not_first)
        def _():
            for c in range(C):
                f_copy(i, c).wait_recv()

        attention_part(i)

        @pl.when(i == 0)
        def _():
            w_copy(0).wait()

        sums(1)
        up_part(0)
        sums(2)
        up_part(1)

        @pl.when(i == 0)
        def _():
            w_copy(1).wait()
            w_copy(2).wait()

        sums(3)
        for c in range(C):
            back_chunk(i, c)
            sums(4 + c)

        @pl.when(jnp.logical_and(relays, i >= delay))
        def _():
            relay(i - delay)

        return carry

    lax.fori_loop(0, n_micro, body, 0)
    last = n_micro - 1
    for c in range(C):
        finish_chunk(last, c)

    @pl.when(not_last)
    def _():
        for m in (n_micro - 2, n_micro - 1):
            for c in range(C):
                f_copy(m, c).wait_send()

    @pl.when(is_last)
    def _():
        for m in (n_micro - 2, n_micro - 1):
            for c in range(C):
                b_wait(m, c)

    @pl.when(relays)
    def _():
        def more(m, carry):
            relay(m)
            return carry

        lax.fori_loop(jnp.maximum(n_micro - delay, 0), n_micro, more, 0)
        for c in range(C):
            relay_copy(last, c, 0, st - 1).wait_send()

        @pl.when(two_hop)
        def _():
            for c in range(C):
                relay_copy(last, c, 1, 1).wait_send()

    @pl.when(lax.rem(st, 2) == 0)
    def _():
        def leaf(m, carry):
            for c in range(C):
                y_wait(m, c)
            return carry

        lax.fori_loop(0, n_micro, leaf, 0)


def copy_kernel(n, src_hbm, dst_hbm, buf, in_sem, out_sem):
    loads = [pltpu.make_async_copy(src_hbm.at[m], buf.at[m], in_sem.at[m]) for m in range(n)]
    stores = [pltpu.make_async_copy(buf.at[m], dst_hbm.at[m], out_sem.at[m]) for m in range(n)]
    for cp in loads:
        cp.start()
    for load, store in zip(loads, stores):
        load.wait()
        store.start()
    for cp in stores:
        cp.wait()


def solution(mesh):
    n_st = mesh.shape["pp"]
    in_specs = (P(), P("pp", None), P("pp", None), P("pp", None, "tp", None), P("pp", "tp", None),
                P("pp", "tp", None, None), P("pp", None), P("pp", None), P("pp", None),
                P("pp", None, "tp"), P("pp", "tp"), P("pp", "tp", None), P("pp", None))

    def device_fn(x_micro, ln1_gain, ln1_bias, w_qkv, b_qkv, w_dense, b_dense, ln2_gain, ln2_bias, w_up, b_up, w_down, b_down):
        n_micro, _, seq, d = x_micro.shape
        heads, hd = w_dense.shape[1], w_dense.shape[2]
        ffn = w_up.shape[2]
        cos_l, sin_lo, sin_hi = rotary_lanes(seq, hd)
        dims = (n_micro, n_st, seq, d, heads, hd, ffn)
        vm = pl.BlockSpec(memory_space=pltpu.VMEM)
        hbm = pl.BlockSpec(memory_space=pl.ANY)
        dma = pltpu.SemaphoreType.DMA
        S, C = X_SLOTS, CHUNKS
        out = pl.pallas_call(
            functools.partial(kernel, dims),
            out_shape=jax.ShapeDtypeStruct((n_micro, seq, d), BF16),
            in_specs=[hbm] + [vm] * 11 + [hbm] * 4,
            out_specs=hbm,
            scratch_shapes=[
                pltpu.VMEM((2, K_BLOCK, heads, 3 * hd), BF16), pltpu.VMEM((3 * hd // 128, K_BLOCK * heads, 128), F32),
                pltpu.VMEM((d, heads * 3 * hd), BF16), pltpu.VMEM((heads * hd, d), BF16),
                pltpu.VMEM((d, ffn), BF16), pltpu.VMEM((ffn, d), BF16),
                pltpu.VMEM((S, seq, d), BF16), pltpu.VMEM((2, seq, d), BF16), pltpu.VMEM((2, seq, d), BF16),
                pltpu.VMEM((2, seq, d), BF16),
                pltpu.VMEM((seq, d), BF16), pltpu.VMEM((seq, d), BF16),
                pltpu.VMEM((seq, heads * 3 * hd), BF16), pltpu.VMEM((heads, seq, seq), BF16), pltpu.VMEM((seq, heads * hd), BF16), pltpu.VMEM((seq, ffn), BF16),
                pltpu.VMEM((1, d), F32), pltpu.VMEM((1, d), F32), pltpu.VMEM((1, d), F32), pltpu.VMEM((1, d), F32),
                pltpu.VMEM((1, heads * 3 * hd), F32), pltpu.VMEM((1, ffn), F32), pltpu.VMEM((1, d), F32),
                dma((3,)), dma((2,)), dma((S,)), dma((S, C)), pltpu.SemaphoreType.REGULAR,
                dma((2, C)), dma((2, C)), dma((2, C)), dma((2, 4, C)), dma((2, C)), dma((n_micro, C)),
            ],
            compiler_params=pltpu.CompilerParams(has_side_effects=True, vmem_limit_bytes=67_043_328),
            name="neox_pipeline",
        )(x_micro.reshape(n_micro, seq, d), jnp.asarray(cos_l), jnp.asarray(sin_lo), jnp.asarray(sin_hi),
          ln1_gain, ln1_bias, ln2_gain, ln2_bias, b_qkv[0], b_up, b_dense, b_down,
          w_qkv[0], w_dense.reshape(heads * hd, d), w_up[0], w_down[0])
        out = pl.pallas_call(functools.partial(copy_kernel, n_micro), out_shape=jax.ShapeDtypeStruct(out.shape, BF16),
                             in_specs=[hbm], out_specs=hbm,
                             scratch_shapes=[pltpu.VMEM(out.shape, BF16), dma((n_micro,)), dma((n_micro,))],
                             compiler_params=pltpu.CompilerParams(vmem_limit_bytes=40_000_000), name="result_copy")(out)
        return out.reshape(x_micro.shape)

    return jax.shard_map(device_fn, mesh=mesh, in_specs=in_specs, out_specs=P(), check_vma=False)
```

time: 1200 us -> 729 us (0.61)
  Pallas kernels: 1170 us -> 729 us
  local copies, waits for them, and re-layouts: 34.2 us -> 0 us
    pallas_call x1, Pallas kernels: 1170 us -> 712 us  [device_fn(): pl.pallas_call(functools.partial(kernel, dims), out_shape=jax.ShapeDtypeS...]
    unnamed x3 -> x0, local copies, waits for them, and re-layouts: 34.2 us -> none
    pallas_call x0 -> x1, Pallas kernels: none -> 17.6 us  [device_fn(): pl.pallas_call(functools.partial(copy_kernel, n_micro), out_shape=jax.Sha...]
where the time goes in v2:
time: 729 us
  Pallas kernels  729 us (100%)
    pallas_call x1, Pallas kernels, device_fn(): pl.pallas_call(functools.partial(kernel, dims), out_shape=jax.ShapeDtypeS...  712 us
    pallas_call x1, Pallas kernels, device_fn(): pl.pallas_call(functools.partial(copy_kernel, n_micro), out_shape=jax.Sha...  17.6 us

profile of v2, /device:TPU:0, one launch (start us, length us, event | category | flops | bytes accessed | tf_op | source)
XLA Modules:
  0.0 729.2 jit_solution(14161337645337950108)
XLA Ops:
  0.0 711.6 %neox_pipeline.1.src_hbm = bf16[48,128,2048]{2,1,0:T(8,128)(2,1)} custom-call(bf16[48,128,2048]{2,1,0:T(8,128)(2,1)} %bitcast.9, f32[128,128]{1,0:T(8,128)} %constant.6.clone.cos_ref, f32[128,128]{1,0:T(8,128)} %constant.7.clone.slo_ref, f32[128,128]{1,0:T(8,128)} %constant.8.clone.shi_ref, bf16[1,2048]{1,0:T(2,128)(2,1)} %g1_ref.1, bf16[1,2048]{1,0:T(2,128)(2,1)} %b1_ref.1, ...), custom_call_target="tpu_custom_call" | custom-call | tf_op jit(solution)/shard_map/neox_pipeline/pallas_call | solution.py:374
  711.6 17.6 %result_copy.1 = bf16[48,128,2048]{2,1,0:T(8,128)(2,1)} custom-call(bf16[48,128,2048]{2,1,0:T(8,128)(2,1)} %neox_pipeline.1.src_hbm), custom_call_target="tpu_custom_call" | custom-call | tf_op jit(solution)/shard_map/result_copy/pallas_call | solution.py:397

commit v3 on v2

--- a/solution.py
+++ b/solution.py
@@ -187,6 +187,24 @@
                 def _():
                     x_load(m + S).start()
 
+    lane = lax.broadcasted_iota(jnp.int32, (seq, hd), 1)
+    rot = hd // 4
+    def rotate(v):
+        v = v.astype(F32)
+        mixed = v * cos_ref[...] + (pltpu.roll(v, hd - rot // 2, 1) * slo_ref[...] + pltpu.roll(v, rot // 2, 1) * shi_ref[...])
+        return jnp.where(lane < rot, mixed, v).astype(BF16)
+
+    causal = lax.broadcasted_iota(jnp.int32, (seq, seq), 0) >= lax.broadcasted_iota(jnp.int32, (seq, seq), 1)
+    def head_probs(h):
+        base = h * 3 * hd
+        query = rotate(qkv[:, pl.ds(base, hd)])
+        key = rotate(qkv[:, pl.ds(base + hd, hd)])
+        scores = lax.dot_general(query, key, (((1,), (1,)), ((), ())), preferred_element_type=F32) * hd ** -0.5
+        scores = jnp.where(causal, scores, -1e30)
+        top = jnp.max(scores, axis=-1, keepdims=True)
+        e = jnp.exp(scores - top)
+        probs[h] = (e / jnp.sum(e, axis=-1, keepdims=True)).astype(BF16)
+
     def attention_part(i):
         xs = lax.rem(i, S)
         rows_per = 16
@@ -201,30 +219,11 @@
 
         a = a_ref[...]
         qw = 2 * 3 * hd
-        lane = lax.broadcasted_iota(jnp.int32, (seq, hd), 1)
-        rot = hd // 4
-        def rotate(v):
-            v = v.astype(F32)
-            mixed = v * cos_ref[...] + (pltpu.roll(v, hd - rot // 2, 1) * slo_ref[...] + pltpu.roll(v, rot // 2, 1) * shi_ref[...])
-            return jnp.where(lane < rot, mixed, v).astype(BF16)
-
-        causal = lax.broadcasted_iota(jnp.int32, (seq, seq), 0) >= lax.broadcasted_iota(jnp.int32, (seq, seq), 1)
-        def head_probs(h):
-            base = h * 3 * hd
-            query = rotate(qkv[:, pl.ds(base, hd)])
-            key = rotate(qkv[:, pl.ds(base + hd, hd)])
-            scores = lax.dot_general(query, key, (((1,), (1,)), ((), ())), preferred_element_type=F32) * hd ** -0.5
-            scores = jnp.where(causal, scores, -1e30)
-            top = jnp.max(scores, axis=-1, keepdims=True)
-            e = jnp.exp(scores - top)
-            probs[h] = (e / jnp.sum(e, axis=-1, keepdims=True)).astype(BF16)
-
         n_q = heads * 3 * hd // qw
-        for q in range(n_q + 1):
-            if q < n_q:
-                cs = pl.ds(q * qw, qw)
-                part = jnp.dot(a, wqkv[:, cs], preferred_element_type=F32)
-                qkv[:, cs] = (part + bqkv[:, cs]).astype(BF16)
+        for q in range(n_q):
+            cs = pl.ds(q * qw, qw)
+            part = jnp.dot(a, wqkv[:, cs], preferred_element_type=F32)
+            qkv[:, cs] = (part + bqkv[:, cs]).astype(BF16)
             if q > 0:
                 for h in range(2 * (q - 1), 2 * q):
                     head_probs(h)
@@ -239,16 +238,23 @@
             gelu = 0.5 * up * (1.0 + lax.erf(up * np.float32(np.sqrt(0.5))))
             hid[:, cs] = gelu.astype(BF16)
             n_u = ffn // uw
+            if u == 0:
+                for h in (heads - 2, heads - 1):
+                    head_probs(h)
             for h in range(heads):
                 if u == min(1 + h * n_u // heads, n_u - 1):
                     value = qkv[:, pl.ds(h * 3 * hd + 2 * hd, hd)]
                     ctx[:, pl.ds(h * hd, hd)] = jnp.dot(probs[h], value, preferred_element_type=F32).astype(BF16)
 
-    def back_chunk(i, c):
-        part = jnp.dot(hid[...], wdn[:, cols(c)], preferred_element_type=F32)
-        part = part + jnp.dot(ctx[...], wd[:, cols(c)], preferred_element_type=F32)
-        psend[lax.rem(i, 2), :, cols(c)] = part.astype(BF16)
+    def attn_out(c):
+        return jnp.dot(ctx[...], wd[:, cols(c)], preferred_element_type=F32)
+
+    def back_chunk(i, c, attn):
+        mlp = jnp.dot(hid[...], wdn[:, cols(c)], preferred_element_type=F32)
+        attn_next = attn_out(c + 1) if c + 1 < C else None
+        psend[lax.rem(i, 2), :, cols(c)] = (mlp + attn).astype(BF16)
         p_copy(i, c).start()
+        return attn_next
 
     lax.fori_loop(0, n_kb, lay_out, 0)
     w_copy(1).start()
@@ -291,8 +297,9 @@
             w_copy(2).wait()
 
         sums(3)
+        attn = attn_out(0)
         for c in range(C):
-            back_chunk(i, c)
+            attn = back_chunk(i, c, attn)
             sums(4 + c)
 
         @pl.when(jnp.logical_and(relays, i >= delay))
@@ -344,12 +351,15 @@
 
 
 def copy_kernel(n, src_hbm, dst_hbm, buf, in_sem, out_sem):
-    loads = [pltpu.make_async_copy(src_hbm.at[m], buf.at[m], in_sem.at[m]) for m in range(n)]
-    stores = [pltpu.make_async_copy(buf.at[m], dst_hbm.at[m], out_sem.at[m]) for m in range(n)]
+    blk = n // in_sem.shape[0]
+    parts = [pl.ds(k * blk, blk) for k in range(n // blk)]
+    loads = [pltpu.make_async_copy(src_hbm.at[p], buf.at[p], in_sem.at[k]) for k, p in enumerate(parts)]
+    stores = [pltpu.make_async_copy(buf.at[p], dst_hbm.at[p], out_sem.at[k]) for k, p in enumerate(parts)]
     for cp in loads:
         cp.start()
     for load, store in zip(loads, stores):
         load.wait()
+    for store in stores:
         store.start()
     for cp in stores:
         cp.wait()
@@ -396,7 +406,7 @@
           w_qkv[0], w_dense.reshape(heads * hd, d), w_up[0], w_down[0])
         out = pl.pallas_call(functools.partial(copy_kernel, n_micro), out_shape=jax.ShapeDtypeStruct(out.shape, BF16),
                              in_specs=[hbm], out_specs=hbm,
-                             scratch_shapes=[pltpu.VMEM(out.shape, BF16), dma((n_micro,)), dma((n_micro,))],
+                             scratch_shapes=[pltpu.VMEM(out.shape, BF16), dma((n_micro // 2,)), dma((n_micro // 2,))],
                              compiler_params=pltpu.CompilerParams(vmem_limit_bytes=40_000_000), name="result_copy")(out)
         return out.reshape(x_micro.shape)
 

time: 729 us -> 727 us (level)
  no operation moved by 1% of the time
where the time goes in v3:
time: 727 us; the launch traced here: 726 us
  Pallas kernels  726 us (100%)
    pallas_call x1, Pallas kernels, device_fn(): pl.pallas_call(functools.partial(kernel, dims), out_shape=jax.ShapeDtypeS...  710 us
    pallas_call x1, Pallas kernels, device_fn(): pl.pallas_call(functools.partial(copy_kernel, n_micro), out_shape=jax.Sha...  16.9 us

profile of v3, /device:TPU:0, one launch (start us, length us, event | category | flops | bytes accessed | tf_op | source)
XLA Modules:
  0.0 726.5 jit_solution(4198638051914654739)
XLA Ops:
  0.0 709.5 %neox_pipeline.1.src_hbm = bf16[48,128,2048]{2,1,0:T(8,128)(2,1)} custom-call(bf16[48,128,2048]{2,1,0:T(8,128)(2,1)} %bitcast.9, f32[128,128]{1,0:T(8,128)} %constant.6.clone.cos_ref, f32[128,128]{1,0:T(8,128)} %constant.7.clone.slo_ref, f32[128,128]{1,0:T(8,128)} %constant.8.clone.shi_ref, bf16[1,2048]{1,0:T(2,128)(2,1)} %g1_ref.1, bf16[1,2048]{1,0:T(2,128)(2,1)} %b1_ref.1, ...), custom_call_target="tpu_custom_call" | custom-call | tf_op jit(solution)/shard_map/neox_pipeline/pallas_call | solution.py:384
  709.5 16.9 %result_copy.1 = bf16[48,128,2048]{2,1,0:T(8,128)(2,1)} custom-call(bf16[48,128,2048]{2,1,0:T(8,128)(2,1)} %neox_pipeline.1.src_hbm), custom_call_target="tpu_custom_call" | custom-call | tf_op jit(solution)/shard_map/result_copy/pallas_call | solution.py:407
